TPU v7x, 256 devices: a whole 4x4x8 slice. The times are simulated.
256 devices in a mesh: span: 16 (over x, z_hi), tensor: 16 (over z_lo, y, core).
Axes of the slice: x: 4, y: 4, z: 8 (z_hi: 4, z_lo: 2; z = z_hi * 2 + z_lo), core: 2. Of those that a mesh axis runs over, the one named last changes fastest.
Arguments:
- latents: bfloat16 [2048, 5120], P(('span', 'tensor')), may hold values from -6 to 6
- modulation: float32 [4, 3, 5120], replicated, may hold values from -3 to 3
- w_query: bfloat16 [5120, 4096], P(None, 'tensor'), may hold values from -0.078125 to 0.078125
- w_key: bfloat16 [5120, 4096], P(None, 'tensor'), may hold values from -0.078125 to 0.078125
- w_value: bfloat16 [5120, 4096], P(None, 'tensor'), may hold values from -0.078125 to 0.078125
- w_out: bfloat16 [4096, 5120], P('tensor'), may hold values from -0.5 to 0.5
- cache_k: bfloat16 [4096, 4096], P('span', 'tensor'), may hold values from -800 to 800
- cache_v: bfloat16 [4096, 4096], P('span', 'tensor'), may hold values from -6 to 6
- level_index: int32 [16], P('span'), may hold values from 0 to 3
- rotation: int32 [16], replicated, may hold values from 0 to 15, each once
- cached_tokens: int32 [1], replicated, may hold values from 128 to 4096
Outputs:
- branch: bfloat16 [2048, 5120], P(('span', 'tensor'))
All inputs are finite; a program needn't handle non-finite values.
Results may differ from a plain program's by a relative error of at most 0.019.
Values may be sent and summed in bfloat16 or wider, within the bound.
A program may use at most 64 MiB of HBM per device.

v0:
```python
import jax
import jax.numpy as jnp
from jax import lax
from jax.sharding import PartitionSpec as P

HD = 128


EPSILON = 1e-06


def laid_out(tiles, dim):
    tiles = jnp.moveaxis(tiles, 0, dim)
    dims = tiles.shape
    return tiles.reshape(*dims[:dim], dims[dim] * dims[dim + 1], *dims[dim + 2 :])


def from_everyone(value, axis):
    copies = jnp.broadcast_to(value, (lax.axis_size(axis), *value.shape))
    return lax.all_to_all(copies, axis, split_axis=0, concat_axis=0, tiled=True)


def collect(value, axis, dim):
    return laid_out(from_everyone(value, axis), dim)


def sent_together(arrays, axis, dim, along):
    widths = [a.shape[along] for a in arrays]
    both = jnp.concatenate(arrays, axis=along)
    whole = lax.all_gather(both, axis, axis=dim, tiled=True)
    return tuple(jnp.split(whole, [sum(widths[:k]) for k in range(1, len(widths))], axis=along))


def in_blocks(value, dim, devices):
    dims = value.shape
    tiles = value.reshape(*dims[:dim], devices, dims[dim] // devices, *dims[dim + 1 :])
    return jnp.moveaxis(tiles, dim, 0)


def sent_and_summed(value, axis, dim):
    tiles = in_blocks(value, dim, lax.axis_size(axis))
    arrived = lax.all_to_all(tiles, axis, split_axis=0, concat_axis=0, tiled=True)
    return arrived.astype(jnp.float32).sum(axis=0)


def block_update(running, q_heads, key_block, value_block, key_valid):
    run_max, run_sum, run_acc = running
    head_count = q_heads.shape[1]
    head_size = q_heads.shape[2]
    key_heads = key_block.reshape(key_block.shape[0], head_count, head_size)
    value_heads = value_block.reshape(value_block.shape[0], head_count, head_size)
    scores = jnp.einsum(
        "qhd,khd->hqk", q_heads, key_heads, preferred_element_type=jnp.float32
    ) * head_size ** (-0.5)
    scores = jnp.where(key_valid[None, None, :], scores, -1e30)
    new_max = jnp.maximum(run_max, jnp.max(scores, axis=-1))
    weights = jnp.where(key_valid[None, None, :], jnp.exp(scores - new_max[..., None]), 0.0)
    rescale = jnp.exp(run_max - new_max)
    run_sum = run_sum * rescale + jnp.sum(weights, axis=-1)
    run_acc = run_acc * rescale[..., None] + jnp.einsum(
        "hqk,khd->hqd",
        weights.astype(jnp.bfloat16),
        value_heads,
        preferred_element_type=jnp.float32,
    )
    return (new_max, run_sum, run_acc)


def attend(running, q_heads, key_rows, value_rows, key_valid):
    key_count = key_rows.shape[0]
    block_len = max(2048, -(-key_count // 8))
    for offset in range(0, key_count, block_len):
        key_block = key_rows[offset : offset + block_len]
        value_block = value_rows[offset : offset + block_len]
        valid_block = key_valid[offset : offset + block_len]
        running = lax.cond(
            jnp.any(valid_block),
            lambda state: block_update(state, q_heads, key_block, value_block, valid_block),
            lambda state: state,
            running,
        )
    return running


def body(
    latents,
    modulation,
    w_query,
    w_key,
    w_value,
    w_out,
    cache_k,
    cache_v,
    level_index,
    rotation,
    cached_tokens,
):
    groups = lax.axis_size("span")
    own_index = lax.axis_index("span")
    chooser = (jnp.arange(modulation.shape[0], dtype=jnp.int32) == level_index[0]).astype(
        jnp.float32
    )
    mod_rows = jnp.sum(chooser[:, None, None] * modulation, axis=0)
    shift_row, scale_row, gate_row = (mod_rows[0], mod_rows[1], mod_rows[2])
    row_data = latents.astype(jnp.float32)
    row_mean = jnp.mean(row_data, axis=-1, keepdims=True)
    centred = row_data - row_mean
    row_var = jnp.mean(centred * centred, axis=-1, keepdims=True)
    normed = centred * lax.rsqrt(row_var + EPSILON)
    modulated = (normed * (1.0 + scale_row) + shift_row).astype(jnp.bfloat16)
    shard_piece = collect(modulated, "tensor", 0)
    projected = [
        jnp.dot(shard_piece, weight, preferred_element_type=jnp.float32).astype(jnp.bfloat16)
        for weight in (w_query, w_key, w_value)
    ]
    joined = jnp.concatenate(projected, axis=1)
    inner_width = w_query.shape[1]
    own_query = joined[:, :inner_width]
    own_key = joined[:, inner_width : 2 * inner_width]
    own_value = joined[:, 2 * inner_width :]
    head_count = inner_width // HD
    span_rows = own_query.shape[0]
    q_heads = own_query.reshape(span_rows, head_count, HD)
    group_ids = jnp.arange(groups, dtype=jnp.int32)
    order_own = jnp.sum(jnp.where(group_ids == own_index, rotation, 0))
    live_keys = cached_tokens[0]
    initial = (
        jnp.full((head_count, span_rows), -1e30, jnp.float32),
        jnp.zeros((head_count, span_rows), jnp.float32),
        jnp.zeros((head_count, span_rows, HD), jnp.float32),
    )
    key_rows, value_rows = sent_together((cache_k, cache_v), "span", 0, 1)
    key_index = jnp.arange(key_rows.shape[0], dtype=jnp.int32)
    running = attend(initial, q_heads, key_rows, value_rows, key_index < live_keys)
    key_rows, value_rows = sent_together((own_key, own_value), "span", 0, 1)
    key_index = jnp.arange(key_rows.shape[0], dtype=jnp.int32)
    key_group = key_index // span_rows
    key_order = jnp.sum(
        jnp.where(key_group[:, None] == group_ids[None, :], rotation[None, :], 0), axis=1
    )
    key_valid = key_order <= order_own
    run_max, run_sum, run_acc = attend(running, q_heads, key_rows, value_rows, key_valid)
    attended = (
        (run_acc / run_sum[..., None])
        .transpose(1, 0, 2)
        .reshape(span_rows, inner_width)
        .astype(jnp.bfloat16)
    )
    projection = sent_and_summed(
        jnp.dot(attended, w_out, preferred_element_type=jnp.float32).astype(jnp.bfloat16),
        "tensor",
        0,
    )
    return (gate_row[None, :] * projection).astype(jnp.bfloat16)


def solution(mesh):
    placed = (
        P(("span", "tensor"), None),
        P(),
        P(None, "tensor"),
        P(None, "tensor"),
        P(None, "tensor"),
        P("tensor", None),
        P("span", "tensor"),
        P("span", "tensor"),
        P("span"),
        P(),
        P(),
    )
    return jax.shard_map(
        body, mesh=mesh, in_specs=placed, out_specs=P(("span", "tensor"), None), check_vma=False
    )
```

profile of v0, /device:TPU:1, one launch (start us, length us, event | category | flops | bytes accessed | tf_op | source)
XLA Modules:
  0.0 201.3 jit_solution(3905024449647434932)
XLA Ops:
  6.5 1.2 copy.38
  7.7 1.0 copy.39
  8.7 0.7 pad_maximum_fusion
  10.1 1.0 convert_reduce_fusion.1
  11.2 1.1 fusion.46
  12.3 1.2 multiply_reduce_fusion
  13.6 1.1 fusion.49
  14.8 31.2 %all_to_all.10 = bf16[16,8,5120]{2,1,0:T(8,128)(2,1)S(1)} all-to-all(bf16[16,8,5120]{2,1,0:T(8,128)(2,1)S(1)} %broadcast_in_dim.104), channel_id=1, replica_groups=mesh['span'=16,'tensor'=16] {'tensor'}, dimensions={0} | all-to-all | bytes 2621440 | tf_op jit(solution)/shard_map/all_to_all | solution.py:20
  46.5 1.7 copy-done.3
  52.7 1.3 fusion.54
  54.7 2.7 %fusion.35 = bf16[128,256]{1,0:T(8,128)(2,1)S(1)} fusion(bf16[5120,256]{1,0:T(8,128)(2,1)} %param.19, bf16[16,8,5120]{2,1,0:T(8,128)(2,1)} %copy-done.1), kind=kOutput, calls=%fused_computation.49 | convolution fusion | flops 335577088 | bytes 3997696 | tf_op jit(solution)/shard_map/dot_general | solution.py:113
  57.3 42.7 %all-gather.3.cloned.1.call-done = bf16[4096,512]{0,1:T(8,128)(2,1)} async-done(((bf16[256,512]{0,1:T(8,128)(2,1)}), bf16[4096,512]{0,1:T(8,128)(2,1)}) %all-gather.3.cloned.1.call-update) | async-done | bytes 4194320 | tf_op jit(solution)/shard_map/all_gather | solution.py:30
  100.0 1.7 fusion.60
  101.7 4.3 %conditional.3 = (f32[2,128]{1,0:T(2,128)}, f32[2,128]{1,0:T(2,128)S(1)}, f32[2,128,128]{2,1,0:T(8,128)S(1)}) conditional(s32[]{:T(128)} %convert_element_type.61, () %tuple.26, (pred[2048]{0:T(1024)(128)(4,1)S(1)}, bf16[2048,256]{0,1:T(8,128)(2,1)S(1)}, bf16[128,2,128]{2,1,0:T(2,128)(2,1)S(1)}, bf16[2048,256]{0,1:T(8,128)(2,1)S(1)}) %tuple.27), branch_computations={%region_8.9_spmd, %region_9.0_spmd} | conditional | flops 273187840 | bytes 8602648 | solution.py:76
  102.9 1.3 convolution_add_fusion
  104.1 1.2 fusion.2
  106.0 5.3 %conditional.4 = ((f32[2,128]{1,0:T(2,128)}, f32[2,128]{1,0:T(2,128)S(1)}, f32[2,128,128]{2,1,0:T(8,128)S(1)})) conditional(s32[]{:T(128)} %convert_element_type.60, (f32[2,128]{1,0:T(2,128)}, f32[2,128]{1,0:T(2,128)S(1)}, f32[2,128,128]{2,1,0:T(8,128)S(1)}) %conditional.3, (pred[2048]{0:T(1024)(128)(4,1)S(1)}, bf16[4096,512]{0,1:T(8,128)(2,1)}, ...), branch_computations={%region_12.13_spmd, %region_13.16_spmd} | conditional | flops 273220096 | bytes 12933152 | solution.py:76
  106.0 1.7 fusion.56
  109.4 0.7 multiply_add_fusion
  111.3 48.4 %all-gather.5.cloned.1.call-done = bf16[2048,512]{1,0:T(8,128)(2,1)} async-done(((bf16[128,512]{1,0:T(8,128)(2,1)}), bf16[2048,512]{1,0:T(8,128)(2,1)}) %all-gather.5.cloned.1.call-update) | async-done | bytes 2097168 | tf_op jit(solution)/shard_map/all_gather | solution.py:30
  159.7 8.8 %conditional.5 = (f32[2,128]{1,0:T(2,128)S(1)}, f32[2,128,128]{1,2,0:T(8,128)S(1)}) conditional(s32[]{:T(128)} %convert_element_type.59, (f32[2,128]{1,0:T(2,128)S(1)}, f32[2,128,128]{2,1,0:T(8,128)S(1)}) %tuple.29, (pred[2048]{0:T(1024)(128)(4,1)S(1)}, bf16[2048,512]{1,0:T(8,128)(2,1)}, bf16[128,2,128]{2,1,0:T(2,128)(2,1)S(1)}, ...), branch_computations={%region_16.17_spmd, %region_17.20_spmd} | conditional | flops 273220096 | bytes 17387536 | solution.py:76
  159.7 4.0 %copy.44 = bf16[2048,512]{0,1:T(8,128)(2,1)} copy(bf16[2048,512]{1,0:T(8,128)(2,1)} %get-tuple-element.128) | data formatting | bytes 4194304 | tf_op jit(solution)/shard_map
  163.7 1.7 fusion.58
  169.1 24.5 %all_to_all.11 = bf16[16,8,5120]{2,1,0:T(8,128)(2,1)S(1)} all-to-all(bf16[16,8,5120]{2,1,0:T(8,128)(2,1)S(1)} %fusion.28), channel_id=1, replica_groups=mesh['span'=16,'tensor'=16] {'tensor'}, dimensions={0} | all-to-all | bytes 2621440 | tf_op jit(solution)/shard_map/all_to_all | solution.py:42
  (45 shorter events, 12.6 us)
Async XLA Ops:
  6.5 162.0 %copy-start = (bf16[256,5120]{1,0:T(8,128)(2,1)S(1)}, bf16[256,5120]{1,0:T(8,128)(2,1)}, u32[]{:S(2)}) copy-start(bf16[256,5120]{1,0:T(8,128)(2,1)} %param.22) | copy-start | bytes 7864324
  6.5 93.5 %all-gather.3.cloned.1.call-start = ((), (), s32[]{:S(2)}) async-start(), calls=%async_computation.2 | async-start | bytes 4456448 | tf_op jit(solution)/shard_map/all_gather | solution.py:30
  9.4 150.3 %all-gather.5.cloned.1.call-start = ((), (), s32[]{:S(2)}) async-start(), calls=%async_computation.3 | async-start | bytes 2228224 | tf_op jit(solution)/shard_map/all_gather | solution.py:30
  13.6 32.5 %copy-start.2 = (bf16[5120,256]{1,0:T(8,128)(2,1)S(1)}, bf16[5120,256]{1,0:T(8,128)(2,1)}, u32[]{:S(2)}) copy-start(bf16[5120,256]{1,0:T(8,128)(2,1)} %param.20) | copy-start | bytes 7864324
  46.0 2.7 %copy-start.1 = (bf16[16,8,5120]{2,1,0:T(8,128)(2,1)}, bf16[16,8,5120]{2,1,0:T(8,128)(2,1)S(1)}, u32[]{:S(2)}) copy-start(bf16[16,8,5120]{2,1,0:T(8,128)(2,1)S(1)} %all_to_all.10) | copy-start | bytes 3932164
  46.0 2.2 %copy-start.3 = (bf16[5120,256]{1,0:T(8,128)(2,1)S(1)}, bf16[5120,256]{1,0:T(8,128)(2,1)}, u32[]{:S(2)}) copy-start(bf16[5120,256]{1,0:T(8,128)(2,1)} %param.21) | copy-start | bytes 7864324
  48.2 3.7 %copy-start.4 = (s32[16]{0:T(128)S(1)}, s32[16]{0:T(128)}, u32[]{:S(2)}) copy-start(s32[16]{0:T(128)} %param.26) | copy-start | bytes 196
Sparse Core Ops, SparseCore 0:
  9.7 90.2 all-gather.2
  102.4 57.2 all-gather.4
where the time goes:
time: 202 us; the launch traced here: 201 us
  waiting for transfers between devices  91.1 us (45%)
  blocking collectives  55.6 us (28%)
  between operations  16.7 us (8%)
  other arithmetic  15.7 us (8%)
  local copies, waits for them, and re-layouts  13.7 us (7%)
  matrix products  8.38 us (4%)
    all_gather x2, waiting for transfers between devices, sent_together(): whole = lax.all_gather(both, axis, axis=dim, tiled=True)  91.1 us
    all_to_all x1, blocking collectives, from_everyone(): return lax.all_to_all(copies, axis, split_axis=0, concat_axis=0, tiled=True)  31.2 us
    all_to_all x1, blocking collectives, sent_and_summed(): lax.all_to_all(tiles, axis, split_axis=0, concat_axis=0, tiled=True)  24.5 us
  transfers between devices with their start and end apart: 2, of which 2 were waited for; matrix products, arithmetic and copies ran while one was open for 11% of the time, Pallas kernels for 0%

commit v1 on v0

v1 whole, which is shorter than its diff:
```python
import functools

import jax
import jax.numpy as jnp
from jax import lax
from jax.experimental import pallas as pl
from jax.experimental.pallas import tpu as pltpu
from jax.sharding import PartitionSpec as P

HD = 128
EPSILON = 1e-06
NEG = -1e30
MESH = pl.DeviceIdType.MESH
F32 = jnp.float32
BF16 = jnp.bfloat16
SCALE2 = HD**-0.5 * 1.4426950408889634

D = 5120
HALF = D // 2
XN, ZN, YN = 4, 4, 4
CHIPS = 8
ROWS = 8
CACHE = 256
SPAN = 128
KEYS = XN * (CACHE + SPAN)
CHIP_STEPS = ((0, 1), (0, 3), (1, 0), (1, 1), (1, 3), (0, 2), (1, 2))
GROUPS = ((0, 0), (1, 0), (0, 1), (1, 1))


def kernel(
    latents, modulation, w_query, w_key, w_value, w_out, cache_k, cache_v, level_index, rotation, cached_tokens,
    out_ref,
    x_buf, lhs, mod, scale_rows, shift_rows, w_in, w_o, ck, cv, nk, nv, qb, bias, scores,
    o_send, o_recv, s_send, s_recv, att, p_send, p_recv,
    load_sem, lat_send, lat_recv, fwd_send, ck_send, ck_recv, q_send, q_recv, kv_send, kv_recv,
    wo_send, wo_recv, ot_send, ot_recv, st_send, st_recv, pr_send, pr_recv,
):
    span = lax.axis_index("span")
    tensor = lax.axis_index("tensor")
    x = span // ZN
    zh = span % ZN
    zl = tensor // 8
    y = (tensor // 2) % YN
    core = tensor % 2
    chip = zl * YN + y
    other = 1 - core

    def chip_at(dl, dy):
        return ((zl + dl) % 2) * YN + (y + dy) % YN

    def chip_device(dl, dy, c):
        return (span, chip_at(dl, dy) * 2 + c)

    sibling = (span, chip * 2 + other)

    def x_device(dx):
        return (((x + dx) % XN) * ZN + zh, tensor)

    def z_device(dz, c):
        return (x * ZN + (zh + dz) % ZN, chip * 2 + c)

    def remote(src, dst, send, recv, device):
        return pltpu.make_async_remote_copy(
            src_ref=src, dst_ref=dst, send_sem=send, recv_sem=recv, device_id=device, device_id_type=MESH
        )

    loads = [
        pltpu.make_async_copy(latents, x_buf.at[tensor], load_sem.at[0]),
        pltpu.make_async_copy(cache_k, ck.at[x], load_sem.at[1]),
        pltpu.make_async_copy(cache_v, cv.at[x], load_sem.at[2]),
        pltpu.make_async_copy(modulation, mod, load_sem.at[3]),
        pltpu.make_async_copy(w_query, w_in.at[0], load_sem.at[4]),
        pltpu.make_async_copy(w_key, w_in.at[1], load_sem.at[5]),
        pltpu.make_async_copy(w_value, w_in.at[2], load_sem.at[6]),
        pltpu.make_async_copy(w_out, w_o.at[core], load_sem.at[7]),
    ]
    for copy in loads:
        copy.start()

    barrier = pltpu.get_barrier_semaphore()
    peers = [sibling]
    peers += [chip_device(dl, dy, core) for dl, dy in CHIP_STEPS]
    peers += [x_device(dx) for dx in (1, 2, 3)]
    peers += [z_device(dz, c) for dz in (1, 2, 3) for c in (0, 1)]
    for device in peers:
        pl.semaphore_signal(barrier, inc=1, device_id=device, device_id_type=MESH)

    live = cached_tokens[0]
    lanes = lax.broadcasted_iota(jnp.int32, (ZN, CACHE), 1)
    for xk in range(XN):
        slots = lanes + (xk * ZN + zh) * CACHE
        bias[:, xk * CACHE : (xk + 1) * CACHE] = jnp.where(slots < live, 0.0, NEG)
    for zq in range(ZN):
        order_q = rotation[x * ZN + zq]
        for xk in range(XN):
            seen = jnp.where(rotation[xk * ZN + zh] <= order_q, 0.0, NEG)
            start = XN * CACHE + xk * SPAN
            bias[zq : zq + 1, start : start + SPAN] = jnp.full((1, SPAN), seen, F32)

    loads[0].wait()
    pl.semaphore_wait(barrier, len(peers))

    waits = []

    def send(src, dst, send_sem, recv_sem, device):
        copy = remote(src, dst, send_sem, recv_sem, device)
        copy.start()
        waits.append(copy)

    own_rows = x_buf.at[tensor]
    for k, (dl, dy) in enumerate(CHIP_STEPS):
        send(own_rows, own_rows, lat_send.at[k], lat_recv.at[tensor], chip_device(dl, dy, core))
    send(own_rows, own_rows, fwd_send.at[7], lat_recv.at[tensor], sibling)

    loads[1].wait()
    loads[2].wait()
    for k, dx in enumerate((1, 3, 2)):
        send(ck.at[x], ck.at[x], ck_send.at[2 * k], ck_recv.at[2 * x], x_device(dx))
        send(cv.at[x], cv.at[x], ck_send.at[2 * k + 1], ck_recv.at[2 * x + 1], x_device(dx))

    loads[3].wait()
    level = level_index[0]
    shift_rows[...] = jnp.broadcast_to(mod[level, 0:1, :], (ROWS, D))
    scale_rows[...] = jnp.broadcast_to(1.0 + mod[level, 1:2, :], (ROWS, D))

    def arrived(index):
        remote(x_buf.at[index], x_buf.at[index], lat_send.at[0], lat_recv.at[index], sibling).wait_recv()

    def normalised(index):
        row_data = x_buf[index].astype(F32)
        mean = jnp.sum(row_data, axis=1, keepdims=True) * (1.0 / D)
        centred = row_data - mean
        var = jnp.sum(centred * centred, axis=1, keepdims=True) * (1.0 / D)
        return centred * lax.rsqrt(var + EPSILON) * scale_rows[...] + shift_rows[...]

    def normalise_pair(first_chip, c):
        rows = jnp.concatenate(
            [normalised(first_chip * 2 + c), normalised((first_chip + 1) * 2 + c)], axis=0
        )
        start = pl.multiple_of(c * (CHIPS * ROWS) + first_chip * ROWS, 16)
        lhs[pl.ds(start, 16), :] = rows.astype(BF16)

    def group_chip(dl, dp):
        return ((zl + dl) % 2) * YN + ((y // 2 + dp) % 2) * 2

    def sibling_pair(first):
        arrived(first * 2 + other)
        arrived((first + 1) * 2 + other)
        normalise_pair(first, other)

    for g, (dl, dp) in enumerate(GROUPS):
        first = group_chip(dl, dp)
        if g == 0:
            mate = first + (1 - y % 2)
            members = [mate]
        else:
            members = [first, first + 1]
        for m, member in enumerate(members):
            arrived(member * 2 + core)
            piece = x_buf.at[member * 2 + core]
            k = 0 if g == 0 else 2 * g - 1 + m
            send(piece, piece, fwd_send.at[k], lat_recv.at[member * 2 + core], sibling)
        normalise_pair(first, core)
        if g > 0:
            sibling_pair(group_chip(*GROUPS[g - 1]))
    sibling_pair(group_chip(*GROUPS[3]))

    def project(which):
        return jnp.dot(lhs[...], w_in[which], preferred_element_type=F32).astype(BF16)

    loads[4].wait()
    queries = project(0)
    for h in range(2):
        qb[h, zh] = queries[:, h * HD : (h + 1) * HD]
    for h in range(2):
        for k, dz in enumerate((2, 1, 3)):
            send(qb.at[h, zh], qb.at[h, zh], q_send.at[3 * h + k], q_recv.at[4 * h + zh], z_device(dz, core))

    def send_rows(buf, v, h):
        for k, dx in enumerate((1, 3, 2)):
            slot = 4 * v + 2 * h
            send(
                buf.at[h, x], buf.at[h, x], kv_send.at[3 * (2 * v + h) + k], kv_recv.at[4 * (2 * v + h) + x], x_device(dx)
            )

    loads[5].wait()
    keys = project(1)
    for h in range(2):
        nk[h, x] = keys[:, h * HD : (h + 1) * HD]
    send_rows(nk, 0, 0)
    loads[6].wait()
    values = project(2)
    for h in range(2):
        nv[h, x] = values[:, h * HD : (h + 1) * HD]
    send_rows(nv, 1, 0)
    send_rows(nk, 0, 1)
    send_rows(nv, 1, 1)
    loads[7].wait()
    send(w_o.at[core], w_o.at[core], wo_send, wo_recv, sibling)

    eye = lax.broadcasted_iota(jnp.int32, (SPAN, SPAN), 0) == lax.broadcasted_iota(jnp.int32, (SPAN, SPAN), 1)

    def key_chunk(h, j):
        if j < XN:
            return ck[j, :, h * HD : (h + 1) * HD]
        j -= XN
        return nk[h, 2 * j : 2 * j + 2].reshape(2 * SPAN, HD)

    def value_chunk(h, j):
        if j < XN:
            return cv[j, :, h * HD : (h + 1) * HD]
        j -= XN
        return nv[h, 2 * j : 2 * j + 2].reshape(2 * SPAN, HD)

    chunks = KEYS // 256

    def attend(h, zq):
        q = qb[h, zq]
        top = None
        for j in range(chunks):
            s = lax.dot_general(q, key_chunk(h, j), (((1,), (1,)), ((), ())), preferred_element_type=F32)
            s = s + bias[pl.ds(zq, 1), j * 256 : (j + 1) * 256]
            scores[:, j * 256 : (j + 1) * 256] = s
            best = jnp.maximum(s[:, :128], s[:, 128:])
            top = best if top is None else jnp.maximum(top, best)
        row_max = jnp.max(top, axis=1, keepdims=True)
        total = jnp.zeros((SPAN, 128), F32)
        acc = jnp.zeros((SPAN, HD), F32)
        for j in range(chunks):
            p = jnp.exp2((scores[:, j * 256 : (j + 1) * 256] - row_max) * SCALE2)
            total = total + (p[:, :128] + p[:, 128:])
            acc = acc + jnp.dot(p.astype(BF16), value_chunk(h, j), preferred_element_type=F32)
        row_sum = jnp.sum(total, axis=1, keepdims=True)
        lse = row_max * SCALE2 + jnp.log2(row_sum)
        part = (acc / row_sum).astype(BF16)
        stat = jnp.sum(jnp.where(eye, lse, 0.0), axis=0, keepdims=True)
        return part, stat

    for h in range(2):
        for dx in (1, 3, 2):
            xk = (x + dx) % XN
            if h == 0:
                remote(ck.at[xk], ck.at[xk], ck_send.at[0], ck_recv.at[2 * xk], sibling).wait_recv()
                remote(cv.at[xk], cv.at[xk], ck_send.at[0], ck_recv.at[2 * xk + 1], sibling).wait_recv()
            remote(nk.at[h, xk], nk.at[h, xk], kv_send.at[0], kv_recv.at[4 * h + xk], sibling).wait_recv()
            remote(nv.at[h, xk], nv.at[h, xk], kv_send.at[0], kv_recv.at[8 + 4 * h + xk], sibling).wait_recv()
        for k, dz in enumerate((1, 3, 2, 0)):
            zq = (zh + dz) % ZN
            if dz:
                remote(qb.at[h, zq], qb.at[h, zq], q_send.at[0], q_recv.at[4 * h + zq], sibling).wait_recv()
            part, stat = attend(h, zq)
            rows = CHIPS * ROWS
            s_send[h, zq] = jnp.broadcast_to(stat, (8, SPAN))
            o_send[h, zq, 0] = part[:rows]
            o_send[h, zq, 1] = part[rows:]
            for c in range(2):
                if dz:
                    n = 6 * h + 2 * k + c
                    slot = 8 * h + 2 * zh
                    device = z_device(dz, c)
                    send(o_send.at[h, zq, c], o_recv.at[h, zh, core], ot_send.at[n], ot_recv.at[slot + core], device)
                    send(s_send.at[h, zq], s_recv.at[h, zh, core], st_send.at[n], st_recv.at[slot + core], device)
            if dz == 0:
                send(
                    o_send.at[h, zq, other], o_recv.at[h, zh, core], ot_send.at[12 + h],
                    ot_recv.at[8 * h + 2 * zh + core], sibling,
                )
                send(
                    s_send.at[h, zq], s_recv.at[h, zh, core], st_send.at[12 + h],
                    st_recv.at[8 * h + 2 * zh + core], sibling,
                )
                o_recv[h, zh, core] = o_send[h, zh, core]
                s_recv[h, zh, core] = s_send[h, zh]

    rows = CHIPS * ROWS
    mine = lax.broadcasted_iota(jnp.int32, (rows, SPAN), 1) == core * rows + lax.broadcasted_iota(
        jnp.int32, (rows, SPAN), 0
    )
    for h in range(2):
        for dz in (0, 1, 3, 2):
            zs = (zh + dz) % ZN
            for dc in range(2):
                cs = (core + dc) % 2
                if dz or dc:
                    slot = 8 * h + 2 * zs + cs
                    remote(o_recv.at[h, zs, cs], o_recv.at[h, zs, cs], ot_send.at[0], ot_recv.at[slot], sibling).wait_recv()
                    remote(s_recv.at[h, zs, cs], s_recv.at[h, zs, cs], st_send.at[0], st_recv.at[slot], sibling).wait_recv()
        for cs in range(2):
            lses = [
                jnp.sum(jnp.where(mine, s_recv[h, zs, cs, 0:1, :], 0.0), axis=1, keepdims=True) for zs in range(ZN)
            ]
            best = jnp.maximum(jnp.maximum(lses[0], lses[1]), jnp.maximum(lses[2], lses[3]))
            shares = [jnp.exp2(value - best) for value in lses]
            whole = shares[0] + shares[1] + shares[2] + shares[3]
            summed = sum(shares[zs] * o_recv[h, zs, cs].astype(F32) for zs in range(ZN))
            att[:, (2 * cs + h) * HD : (2 * cs + h + 1) * HD] = (summed / whole).astype(BF16)

    remote(w_o.at[other], w_o.at[other], wo_send, wo_recv, sibling).wait_recv()
    step = 512
    for half in range(2):

        @pl.loop(0, HALF // step)
        def _(n):
            cols = pl.ds(pl.multiple_of(half * HALF + n * step, step), step)
            value = jnp.dot(att[:, : 2 * HD], w_o[0, :, cols], preferred_element_type=F32) + jnp.dot(
                att[:, 2 * HD :], w_o[1, :, cols], preferred_element_type=F32
            )
            p_send[:, :, cols] = value.reshape(CHIPS, ROWS, step).astype(BF16)

        cols = pl.ds(half * HALF, HALF)
        for k, (dl, dy) in enumerate(CHIP_STEPS):
            send(
                p_send.at[chip_at(dl, dy), :, cols], p_recv.at[chip, :, cols], pr_send.at[7 * half + k],
                pr_recv.at[8 * half + chip], chip_device(dl, dy, core),
            )

    gate = mod[level, 2:3, :]
    for half in range(2):
        cols = pl.ds(half * HALF, HALF)
        total = p_send[chip, :, cols].astype(F32)
        for dl, dy in CHIP_STEPS:
            source = chip_at(dl, dy)
            remote(
                p_recv.at[source, :, cols], p_recv.at[source, :, cols], pr_send.at[0], pr_recv.at[8 * half + source],
                sibling,
            ).wait_recv()
            total = total + p_recv[source, :, cols].astype(F32)
        out_ref[:, half * HALF : (half + 1) * HALF] = (gate[:, half * HALF : (half + 1) * HALF] * total).astype(BF16)

    for copy in waits:
        copy.wait_send()


def body(
    latents, modulation, w_query, w_key, w_value, w_out, cache_k, cache_v, level_index, rotation, cached_tokens
):
    anywhere = pl.BlockSpec(memory_space=pl.ANY)
    smem = pl.BlockSpec(memory_space=pltpu.SMEM)
    dma = pltpu.SemaphoreType.DMA
    rows = CHIPS * ROWS
    return pl.pallas_call(
        kernel,
        out_shape=jax.ShapeDtypeStruct((ROWS, D), BF16),
        in_specs=[anywhere] * 8 + [smem] * 3,
        out_specs=pl.BlockSpec(memory_space=pltpu.VMEM),
        scratch_shapes=[
            pltpu.VMEM((16, ROWS, D), BF16),
            pltpu.VMEM((SPAN, D), BF16),
            pltpu.VMEM((4, 3, D), F32),
            pltpu.VMEM((ROWS, D), F32),
            pltpu.VMEM((ROWS, D), F32),
            pltpu.VMEM((3, D, 2 * HD), BF16),
            pltpu.VMEM((2, 2 * HD, D), BF16),
            pltpu.VMEM((XN, CACHE, 2 * HD), BF16),
            pltpu.VMEM((XN, CACHE, 2 * HD), BF16),
            pltpu.VMEM((2, XN, SPAN, HD), BF16),
            pltpu.VMEM((2, XN, SPAN, HD), BF16),
            pltpu.VMEM((2, ZN, SPAN, HD), BF16),
            pltpu.VMEM((ZN, KEYS), F32),
            pltpu.VMEM((SPAN, KEYS), F32),
            pltpu.VMEM((2, ZN, 2, rows, HD), BF16),
            pltpu.VMEM((2, ZN, 2, rows, HD), BF16),
            pltpu.VMEM((2, ZN, 8, SPAN), F32),
            pltpu.VMEM((2, ZN, 2, 8, SPAN), F32),
            pltpu.VMEM((rows, 4 * HD), BF16),
            pltpu.VMEM((CHIPS, ROWS, D), BF16),
            pltpu.VMEM((CHIPS, ROWS, D), BF16),
            dma((8,)),
            dma((7,)),
            dma((16,)),
            dma((8,)),
            dma((6,)),
            dma((8,)),
            dma((6,)),
            dma((8,)),
            dma((12,)),
            dma((16,)),
            dma(()),
            dma(()),
            dma((14,)),
            dma((16,)),
            dma((14,)),
            dma((16,)),
            dma((14,)),
            dma((16,)),
        ],
        compiler_params=pltpu.CompilerParams(
            collective_id=0, has_side_effects=True, vmem_limit_bytes=60 * 1024 * 1024
        ),
        name="attention_step",
    )(latents, modulation, w_query, w_key, w_value, w_out, cache_k, cache_v, level_index, rotation, cached_tokens)


def solution(mesh):
    placed = (
        P(("span", "tensor"), None),
        P(),
        P(None, "tensor"),
        P(None, "tensor"),
        P(None, "tensor"),
        P("tensor", None),
        P("span", "tensor"),
        P("span", "tensor"),
        P("span"),
        P(),
        P(),
    )
    return jax.shard_map(
        body, mesh=mesh, in_specs=placed, out_specs=P(("span", "tensor"), None), check_vma=False
    )
```

time: 202 us -> 59.6 us (0.30)
  waiting for transfers between devices: 91.1 us -> 0 us
  blocking collectives: 55.6 us -> 0 us
  Pallas kernels: 0 us -> 54.8 us
  other arithmetic: 15.7 us -> 0 us
  between operations: 16.7 us -> 1.31 us
  local copies, waits for them, and re-layouts: 13.7 us -> 3.35 us
  matrix products: 8.38 us -> 0 us
    all_gather x2 -> x0, waiting for transfers between devices: 91.1 us -> none  [sent_together(): whole = lax.all_gather(both, axis, axis=dim, tiled=True)]
    all_to_all x2 -> x0, blocking collectives: 55.6 us -> none  [the longest x1 31.2 us: from_everyone(): return lax.all_to_all(copies, axis, split_axis=0, concat_axis=0, tiled=True)]
    pallas_call x0 -> x1, Pallas kernels: none -> 54.8 us  [body(): pl.pallas_call(kernel, out_shape=jax.ShapeDtypeStruct((ROWS, D), BF16), i...]
    dot_general x10 -> x0, matrix products: 8.38 us -> none  [the longest x3 3.67 us: body(): jnp.dot(shard_piece, weight, preferred_element_type=jnp.float32)]
    reduce_sum x9 -> x0, other arithmetic: 6.4 us -> none  [the longest x3 2.15 us: block_update(): run_sum = run_sum * rescale + jnp.sum(weights, axis=-1)]
    another operation x1 -> x0, local copies, waits for them, and re-layouts: 3.98 us -> none
    slice x2 -> x0, local copies, waits for them, and re-layouts: 3.36 us -> none  [attend(): value_block = value_rows[offset:offset + block_len]]
    add x3 -> x0, other arithmetic: 2.08 us -> none  [block_update(): run_sum = run_sum * rescale + jnp.sum(weights, axis=-1)]
  transfers between devices with their start and end apart: 2 -> 0, of which waited for: 2 -> 0; matrix products, arithmetic and copies ran while one was open for 11% -> 0% of each run, Pallas kernels for 0% -> 0%
where the time goes in v1:
time: 59.6 us; the launch traced here: 59.4 us
  Pallas kernels  54.8 us (92%)
  local copies, waits for them, and re-layouts  3.35 us (6%)
  between operations  1.31 us (2%)
    pallas_call x1, Pallas kernels, body(): pl.pallas_call(kernel, out_shape=jax.ShapeDtypeStruct((ROWS, D), BF16), i...  54.8 us
    unnamed x2, local copies, waits for them, and re-layouts  3.35 us

profile of v1, /device:TPU:1, one launch (start us, length us, event | category | flops | bytes accessed | tf_op | source)
XLA Modules:
  0.0 59.4 jit_solution(10459313844307229257)
XLA Ops:
  1.3 1.8 %copy.12.modulation = f32[4,3,5120]{2,1,0:T(4,128)} copy(f32[4,3,5120]{2,0,1:T(4,128)} %param.12) | data formatting | bytes 491520 | tf_op args[1]
  3.1 54.8 %attention_step.1 = bf16[8,5120]{1,0:T(8,128)(2,1)} custom-call(bf16[8,5120]{1,0:T(8,128)(2,1)} %latents.1, f32[4,3,5120]{2,1,0:T(4,128)} %copy.12.modulation, bf16[5120,256]{1,0:T(8,128)(2,1)} %w_query.1, bf16[5120,256]{1,0:T(8,128)(2,1)} %w_key.1, bf16[5120,256]{1,0:T(8,128)(2,1)} %w_value.1, bf16[256,5120]{1,0:T(8,128)(2,1)} %w_out.1, ...), custom_call_target="tpu_custom_call" | custom-call | tf_op jit(solution)/shard_map/attention_step/pallas_call | solution.py:341
  57.9 1.5 %copy.16 = bf16[8,5120]{1,0:T(8,128)(2,1)} copy(bf16[8,5120]{1,0:T(8,128)(2,1)} %attention_step.1) | data formatting | bytes 163840

commit v2 on v1

--- a/solution.py
+++ b/solution.py
@@ -24,13 +24,15 @@
 SPAN = 128
 KEYS = XN * (CACHE + SPAN)
 CHIP_STEPS = ((0, 1), (0, 3), (1, 0), (1, 1), (1, 3), (0, 2), (1, 2))
+PARTS = 4
+WIDTH = D // PARTS
 GROUPS = ((0, 0), (1, 0), (0, 1), (1, 1))
 
 
 def kernel(
     latents, modulation, w_query, w_key, w_value, w_out, cache_k, cache_v, level_index, rotation, cached_tokens,
     out_ref,
-    x_buf, lhs, mod, scale_rows, shift_rows, w_in, w_o, ck, cv, nk, nv, qb, bias, scores,
+    level_s, rot_s, live_s, x_buf, lhs, mod, scale_rows, shift_rows, w_in, w_o, ck, cv, nk, nv, qb, slot_bias, span_bias, v_raw, scores,
     o_send, o_recv, s_send, s_recv, att, p_send, p_recv,
     load_sem, lat_send, lat_recv, fwd_send, ck_send, ck_recv, q_send, q_recv, kv_send, kv_recv,
     wo_send, wo_recv, ot_send, ot_recv, st_send, st_recv, pr_send, pr_recv,
@@ -64,17 +66,22 @@
             src_ref=src, dst_ref=dst, send_sem=send, recv_sem=recv, device_id=device, device_id_type=MESH
         )
 
+    scalars = [
+        pltpu.make_async_copy(level_index, level_s, load_sem.at[8]),
+        pltpu.make_async_copy(rotation, rot_s, load_sem.at[9]),
+        pltpu.make_async_copy(cached_tokens, live_s, load_sem.at[10]),
+    ]
     loads = [
         pltpu.make_async_copy(latents, x_buf.at[tensor], load_sem.at[0]),
         pltpu.make_async_copy(cache_k, ck.at[x], load_sem.at[1]),
-        pltpu.make_async_copy(cache_v, cv.at[x], load_sem.at[2]),
+        pltpu.make_async_copy(cache_v, v_raw, load_sem.at[2]),
         pltpu.make_async_copy(modulation, mod, load_sem.at[3]),
         pltpu.make_async_copy(w_query, w_in.at[0], load_sem.at[4]),
         pltpu.make_async_copy(w_key, w_in.at[1], load_sem.at[5]),
         pltpu.make_async_copy(w_value, w_in.at[2], load_sem.at[6]),
         pltpu.make_async_copy(w_out, w_o.at[core], load_sem.at[7]),
     ]
-    for copy in loads:
+    for copy in loads[:1] + scalars + loads[1:]:
         copy.start()
 
     barrier = pltpu.get_barrier_semaphore()
@@ -85,17 +92,19 @@
     for device in peers:
         pl.semaphore_signal(barrier, inc=1, device_id=device, device_id_type=MESH)
 
-    live = cached_tokens[0]
-    lanes = lax.broadcasted_iota(jnp.int32, (ZN, CACHE), 1)
+    for copy in scalars:
+        copy.wait()
+    live = live_s[0]
+    level = level_s[0]
+    slot = lax.broadcasted_iota(jnp.int32, (CACHE, SPAN), 0)
     for xk in range(XN):
-        slots = lanes + (xk * ZN + zh) * CACHE
-        bias[:, xk * CACHE : (xk + 1) * CACHE] = jnp.where(slots < live, 0.0, NEG)
+        base = (xk * ZN + zh) * CACHE
+        slot_bias[xk * CACHE : (xk + 1) * CACHE] = jnp.where(slot + base < live, 0.0, NEG)
     for zq in range(ZN):
-        order_q = rotation[x * ZN + zq]
+        order_q = rot_s[x * ZN + zq]
         for xk in range(XN):
-            seen = jnp.where(rotation[xk * ZN + zh] <= order_q, 0.0, NEG)
-            start = XN * CACHE + xk * SPAN
-            bias[zq : zq + 1, start : start + SPAN] = jnp.full((1, SPAN), seen, F32)
+            seen = jnp.where(rot_s[xk * ZN + zh] <= order_q, 0.0, NEG)
+            span_bias[zq, xk] = jnp.full((ROWS, SPAN), seen, F32)
 
     loads[0].wait()
     pl.semaphore_wait(barrier, len(peers))
@@ -114,14 +123,14 @@
 
     loads[1].wait()
     loads[2].wait()
+    cv[x] = v_raw[...].T
     for k, dx in enumerate((1, 3, 2)):
         send(ck.at[x], ck.at[x], ck_send.at[2 * k], ck_recv.at[2 * x], x_device(dx))
         send(cv.at[x], cv.at[x], ck_send.at[2 * k + 1], ck_recv.at[2 * x + 1], x_device(dx))
 
     loads[3].wait()
-    level = level_index[0]
-    shift_rows[...] = jnp.broadcast_to(mod[level, 0:1, :], (ROWS, D))
-    scale_rows[...] = jnp.broadcast_to(1.0 + mod[level, 1:2, :], (ROWS, D))
+    shift_rows[...] = jnp.broadcast_to(mod[0, pl.ds(level, 1), :], (ROWS, D))
+    scale_rows[...] = jnp.broadcast_to(1.0 + mod[1, pl.ds(level, 1), :], (ROWS, D))
 
     def arrived(index):
         remote(x_buf.at[index], x_buf.at[index], lat_send.at[0], lat_recv.at[index], sibling).wait_recv()
@@ -166,7 +175,12 @@
     sibling_pair(group_chip(*GROUPS[3]))
 
     def project(which):
-        return jnp.dot(lhs[...], w_in[which], preferred_element_type=F32).astype(BF16)
+        sums = [None, None]
+        for n in range(D // 256):
+            depth = slice(n // 2 * 256 + n % 2 * HALF, (n // 2 + 1) * 256 + n % 2 * HALF)
+            part = jnp.dot(lhs[:, depth], w_in[which, depth], preferred_element_type=F32)
+            sums[n % 2] = part if sums[n % 2] is None else sums[n % 2] + part
+        return (sums[0] + sums[1]).astype(BF16)
 
     loads[4].wait()
     queries = project(0)
@@ -178,7 +192,6 @@
 
     def send_rows(buf, v, h):
         for k, dx in enumerate((1, 3, 2)):
-            slot = 4 * v + 2 * h
             send(
                 buf.at[h, x], buf.at[h, x], kv_send.at[3 * (2 * v + h) + k], kv_recv.at[4 * (2 * v + h) + x], x_device(dx)
             )
@@ -191,15 +204,13 @@
     loads[6].wait()
     values = project(2)
     for h in range(2):
-        nv[h, x] = values[:, h * HD : (h + 1) * HD]
+        nv[h, x] = values[:, h * HD : (h + 1) * HD].T
     send_rows(nv, 1, 0)
     send_rows(nk, 0, 1)
     send_rows(nv, 1, 1)
     loads[7].wait()
     send(w_o.at[core], w_o.at[core], wo_send, wo_recv, sibling)
 
-    eye = lax.broadcasted_iota(jnp.int32, (SPAN, SPAN), 0) == lax.broadcasted_iota(jnp.int32, (SPAN, SPAN), 1)
-
     def key_chunk(h, j):
         if j < XN:
             return ck[j, :, h * HD : (h + 1) * HD]
@@ -208,33 +219,49 @@
 
     def value_chunk(h, j):
         if j < XN:
-            return cv[j, :, h * HD : (h + 1) * HD]
+            return cv[j, h * HD : (h + 1) * HD, :]
         j -= XN
-        return nv[h, 2 * j : 2 * j + 2].reshape(2 * SPAN, HD)
+        return jnp.concatenate([nv[h, 2 * j], nv[h, 2 * j + 1]], axis=1)
+
+    def mask_chunk(zqs, j):
+        if j < XN:
+            tile = slot_bias[j * CACHE : (j + 1) * CACHE]
+            return jnp.concatenate([tile] * len(zqs), axis=1)
+        j -= XN
+        rows = []
+        for xk in (2 * j, 2 * j + 1):
+            tile = jnp.concatenate([span_bias[zq, xk] for zq in zqs], axis=1)
+            rows.append(jnp.broadcast_to(tile[None], (SPAN // ROWS, *tile.shape)).reshape(SPAN, -1))
+        return jnp.concatenate(rows, axis=0)
 
     chunks = KEYS // 256
 
-    def attend(h, zq):
-        q = qb[h, zq]
+    def attend(h, zqs):
+        width = len(zqs) * SPAN
+        q = jnp.concatenate([qb[h, zq] for zq in zqs], axis=0)
         top = None
         for j in range(chunks):
-            s = lax.dot_general(q, key_chunk(h, j), (((1,), (1,)), ((), ())), preferred_element_type=F32)
-            s = s + bias[pl.ds(zq, 1), j * 256 : (j + 1) * 256]
-            scores[:, j * 256 : (j + 1) * 256] = s
-            best = jnp.maximum(s[:, :128], s[:, 128:])
+            s = lax.dot_general(key_chunk(h, j), q, (((1,), (1,)), ((), ())), preferred_element_type=F32)
+            s = s + mask_chunk(zqs, j)
+            scores[j * 256 : (j + 1) * 256] = s
+            best = jnp.max(s.reshape(256 // ROWS, ROWS, width), axis=0)
             top = best if top is None else jnp.maximum(top, best)
-        row_max = jnp.max(top, axis=1, keepdims=True)
-        total = jnp.zeros((SPAN, 128), F32)
-        acc = jnp.zeros((SPAN, HD), F32)
+        top = jnp.max(top, axis=0, keepdims=True)
+        acc = total = None
         for j in range(chunks):
-            p = jnp.exp2((scores[:, j * 256 : (j + 1) * 256] - row_max) * SCALE2)
-            total = total + (p[:, :128] + p[:, 128:])
-            acc = acc + jnp.dot(p.astype(BF16), value_chunk(h, j), preferred_element_type=F32)
-        row_sum = jnp.sum(total, axis=1, keepdims=True)
-        lse = row_max * SCALE2 + jnp.log2(row_sum)
-        part = (acc / row_sum).astype(BF16)
-        stat = jnp.sum(jnp.where(eye, lse, 0.0), axis=0, keepdims=True)
-        return part, stat
+            p = jnp.exp2((scores[j * 256 : (j + 1) * 256] - top) * SCALE2)
+            share = jnp.sum(p.reshape(256 // ROWS, ROWS, width), axis=0)
+            part = jnp.dot(value_chunk(h, j), p.astype(BF16), preferred_element_type=F32)
+            total = share if total is None else total + share
+            acc = part if acc is None else acc + part
+        total = jnp.sum(total, axis=0, keepdims=True)
+        lse = top * SCALE2 + jnp.log2(total)
+        acc = acc / total
+        out = []
+        for n in range(len(zqs)):
+            cols = slice(n * SPAN, (n + 1) * SPAN)
+            out.append((acc[:, cols].T.astype(BF16), lse[:, cols]))
+        return out
 
     for h in range(2):
         for dx in (1, 3, 2):
@@ -244,11 +271,17 @@
                 remote(cv.at[xk], cv.at[xk], ck_send.at[0], ck_recv.at[2 * xk + 1], sibling).wait_recv()
             remote(nk.at[h, xk], nk.at[h, xk], kv_send.at[0], kv_recv.at[4 * h + xk], sibling).wait_recv()
             remote(nv.at[h, xk], nv.at[h, xk], kv_send.at[0], kv_recv.at[8 + 4 * h + xk], sibling).wait_recv()
+        results = []
         for k, dz in enumerate((1, 3, 2, 0)):
             zq = (zh + dz) % ZN
-            if dz:
-                remote(qb.at[h, zq], qb.at[h, zq], q_send.at[0], q_recv.at[4 * h + zq], sibling).wait_recv()
-            part, stat = attend(h, zq)
+            if k % 2 == 0:
+                pair = [1, 3] if k == 0 else [2, 0]
+                zqs = [(zh + d) % ZN for d in pair]
+                for d, z in zip(pair, zqs):
+                    if d:
+                        remote(qb.at[h, z], qb.at[h, z], q_send.at[0], q_recv.at[4 * h + z], sibling).wait_recv()
+                results += attend(h, zqs)
+            part, stat = results[k]
             rows = CHIPS * ROWS
             s_send[h, zq] = jnp.broadcast_to(stat, (8, SPAN))
             o_send[h, zq, 0] = part[:rows]
@@ -296,36 +329,30 @@
             att[:, (2 * cs + h) * HD : (2 * cs + h + 1) * HD] = (summed / whole).astype(BF16)
 
     remote(w_o.at[other], w_o.at[other], wo_send, wo_recv, sibling).wait_recv()
-    step = 512
-    for half in range(2):
-
-        @pl.loop(0, HALF // step)
-        def _(n):
-            cols = pl.ds(pl.multiple_of(half * HALF + n * step, step), step)
-            value = jnp.dot(att[:, : 2 * HD], w_o[0, :, cols], preferred_element_type=F32) + jnp.dot(
-                att[:, 2 * HD :], w_o[1, :, cols], preferred_element_type=F32
-            )
-            p_send[:, :, cols] = value.reshape(CHIPS, ROWS, step).astype(BF16)
-
-        cols = pl.ds(half * HALF, HALF)
+    for part in range(PARTS):
+        cols = pl.ds(part * WIDTH, WIDTH)
+        value = jnp.dot(att[:, : 2 * HD], w_o[0, :, cols], preferred_element_type=F32) + jnp.dot(
+            att[:, 2 * HD :], w_o[1, :, cols], preferred_element_type=F32
+        )
+        p_send[:, :, cols] = value.reshape(CHIPS, ROWS, WIDTH).astype(BF16)
         for k, (dl, dy) in enumerate(CHIP_STEPS):
             send(
-                p_send.at[chip_at(dl, dy), :, cols], p_recv.at[chip, :, cols], pr_send.at[7 * half + k],
-                pr_recv.at[8 * half + chip], chip_device(dl, dy, core),
+                p_send.at[chip_at(dl, dy), :, cols], p_recv.at[chip, :, cols], pr_send.at[7 * part + k],
+                pr_recv.at[8 * part + chip], chip_device(dl, dy, core),
             )
 
-    gate = mod[level, 2:3, :]
-    for half in range(2):
-        cols = pl.ds(half * HALF, HALF)
+    gate = mod[2, pl.ds(level, 1), :]
+    for part in range(PARTS):
+        cols = pl.ds(part * WIDTH, WIDTH)
         total = p_send[chip, :, cols].astype(F32)
         for dl, dy in CHIP_STEPS:
             source = chip_at(dl, dy)
             remote(
-                p_recv.at[source, :, cols], p_recv.at[source, :, cols], pr_send.at[0], pr_recv.at[8 * half + source],
+                p_recv.at[source, :, cols], p_recv.at[source, :, cols], pr_send.at[0], pr_recv.at[8 * part + source],
                 sibling,
             ).wait_recv()
             total = total + p_recv[source, :, cols].astype(F32)
-        out_ref[:, half * HALF : (half + 1) * HALF] = (gate[:, half * HALF : (half + 1) * HALF] * total).astype(BF16)
+        out_ref[:, cols] = (gate[:, part * WIDTH : (part + 1) * WIDTH] * total).astype(BF16)
 
     for copy in waits:
         copy.wait_send()
@@ -334,30 +361,34 @@
 def body(
     latents, modulation, w_query, w_key, w_value, w_out, cache_k, cache_v, level_index, rotation, cached_tokens
 ):
-    anywhere = pl.BlockSpec(memory_space=pl.ANY)
-    smem = pl.BlockSpec(memory_space=pltpu.SMEM)
+    anywhere = pl.BlockSpec(memory_space=pltpu.HBM)
     dma = pltpu.SemaphoreType.DMA
     rows = CHIPS * ROWS
     return pl.pallas_call(
         kernel,
         out_shape=jax.ShapeDtypeStruct((ROWS, D), BF16),
-        in_specs=[anywhere] * 8 + [smem] * 3,
+        in_specs=[anywhere] * 11,
         out_specs=pl.BlockSpec(memory_space=pltpu.VMEM),
         scratch_shapes=[
+            pltpu.SMEM((1,), jnp.int32),
+            pltpu.SMEM((16,), jnp.int32),
+            pltpu.SMEM((1,), jnp.int32),
             pltpu.VMEM((16, ROWS, D), BF16),
             pltpu.VMEM((SPAN, D), BF16),
-            pltpu.VMEM((4, 3, D), F32),
+            pltpu.VMEM((3, 4, D), F32),
             pltpu.VMEM((ROWS, D), F32),
             pltpu.VMEM((ROWS, D), F32),
             pltpu.VMEM((3, D, 2 * HD), BF16),
             pltpu.VMEM((2, 2 * HD, D), BF16),
             pltpu.VMEM((XN, CACHE, 2 * HD), BF16),
-            pltpu.VMEM((XN, CACHE, 2 * HD), BF16),
+            pltpu.VMEM((XN, 2 * HD, CACHE), BF16),
             pltpu.VMEM((2, XN, SPAN, HD), BF16),
-            pltpu.VMEM((2, XN, SPAN, HD), BF16),
+            pltpu.VMEM((2, XN, HD, SPAN), BF16),
             pltpu.VMEM((2, ZN, SPAN, HD), BF16),
-            pltpu.VMEM((ZN, KEYS), F32),
-            pltpu.VMEM((SPAN, KEYS), F32),
+            pltpu.VMEM((XN * CACHE, SPAN), F32),
+            pltpu.VMEM((ZN, XN, ROWS, SPAN), F32),
+            pltpu.VMEM((CACHE, 2 * HD), BF16),
+            pltpu.VMEM((KEYS, 2 * SPAN), F32),
             pltpu.VMEM((2, ZN, 2, rows, HD), BF16),
             pltpu.VMEM((2, ZN, 2, rows, HD), BF16),
             pltpu.VMEM((2, ZN, 8, SPAN), F32),
@@ -365,7 +396,7 @@
             pltpu.VMEM((rows, 4 * HD), BF16),
             pltpu.VMEM((CHIPS, ROWS, D), BF16),
             pltpu.VMEM((CHIPS, ROWS, D), BF16),
-            dma((8,)),
+            dma((11,)),
             dma((7,)),
             dma((16,)),
             dma((8,)),
@@ -381,14 +412,14 @@
             dma((16,)),
             dma((14,)),
             dma((16,)),
-            dma((14,)),
-            dma((16,)),
+            dma((7 * PARTS,)),
+            dma((8 * PARTS,)),
         ],
         compiler_params=pltpu.CompilerParams(
             collective_id=0, has_side_effects=True, vmem_limit_bytes=60 * 1024 * 1024
         ),
         name="attention_step",
-    )(latents, modulation, w_query, w_key, w_value, w_out, cache_k, cache_v, level_index, rotation, cached_tokens)
+    )(latents, jnp.transpose(modulation, (1, 0, 2)), w_query, w_key, w_value, w_out, cache_k, cache_v, level_index, rotation, cached_tokens)
 
 
 def solution(mesh):

time: 59.6 us -> 56.2 us (0.943)
  local copies, waits for them, and re-layouts: 3.35 us -> 1.53 us
  Pallas kernels: 54.8 us -> 53.2 us
    unnamed x2 -> x1, local copies, waits for them, and re-layouts: 3.35 us -> 1.53 us
    pallas_call x1, Pallas kernels: 54.8 us -> 53.2 us  [body(): pl.pallas_call(kernel, out_shape=jax.ShapeDtypeStruct((ROWS, D), BF16), i...]
where the time goes in v2:
time: 56.2 us; the launch traced here: 56 us
  Pallas kernels  53.2 us (95%)
  local copies, waits for them, and re-layouts  1.53 us (3%)
  between operations  1.3 us (2%)
    pallas_call x1, Pallas kernels, body(): pl.pallas_call(kernel, out_shape=jax.ShapeDtypeStruct((ROWS, D), BF16), i...  53.2 us
    unnamed x1, local copies, waits for them, and re-layouts  1.53 us

profile of v2, /device:TPU:1, one launch (start us, length us, event | category | flops | bytes accessed | tf_op | source)
XLA Modules:
  0.0 56.0 jit_solution(16929202462398170428)
XLA Ops:
  1.3 53.2 %attention_step.1 = bf16[8,5120]{1,0:T(8,128)(2,1)} custom-call(bf16[8,5120]{1,0:T(8,128)(2,1)} %latents.1, f32[3,4,5120]{2,1,0:T(4,128)} %bitcast.1, bf16[5120,256]{1,0:T(8,128)(2,1)} %w_query.1, bf16[5120,256]{1,0:T(8,128)(2,1)} %w_key.1, bf16[5120,256]{1,0:T(8,128)(2,1)} %w_value.1, bf16[256,5120]{1,0:T(8,128)(2,1)} %w_out.1, bf16[256,256]{1,0:T(8,128)(2,1)} %cache_k.1, ...), custom_call_target="tpu_custom_call" | custom-call | tf_op jit(solution)/shard_map/attention_step/pallas_call | solution.py:367
  54.5 1.5 %copy.15 = bf16[8,5120]{1,0:T(8,128)(2,1)} copy(bf16[8,5120]{1,0:T(8,128)(2,1)} %attention_step.1) | data formatting | bytes 163840

commit v3 on v2

--- a/solution.py
+++ b/solution.py
@@ -23,19 +23,19 @@
 CACHE = 256
 SPAN = 128
 KEYS = XN * (CACHE + SPAN)
-CHIP_STEPS = ((0, 1), (0, 3), (1, 0), (1, 1), (1, 3), (0, 2), (1, 2))
+NEAR = ((0, 1), (0, 3), (1, 1), (1, 3), (1, 0))
 PARTS = 4
 WIDTH = D // PARTS
-GROUPS = ((0, 0), (1, 0), (0, 1), (1, 1))
 
 
 def kernel(
     latents, modulation, w_query, w_key, w_value, w_out, cache_k, cache_v, level_index, rotation, cached_tokens,
     out_ref,
-    level_s, rot_s, live_s, x_buf, lhs, mod, scale_rows, shift_rows, w_in, w_o, ck, cv, nk, nv, qb, slot_bias, span_bias, v_raw, scores,
-    o_send, o_recv, s_send, s_recv, att, p_send, p_recv,
-    load_sem, lat_send, lat_recv, fwd_send, ck_send, ck_recv, q_send, q_recv, kv_send, kv_recv,
-    wo_send, wo_recv, ot_send, ot_recv, st_send, st_recv, pr_send, pr_recv,
+    level_s, rot_s, live_s, x_buf, lhs, mod, scale_rows, shift_rows, w_in, w_o, ck, cv, nk, nv, qb, slot_bias, span_bias, v_raw, scores, probs,
+    o_send, o_recv, s_send, s_recv, att, p_send, p_recv, p_sum, hop_recv,
+    load_sem, lat_send, lat_recv, far_send, far_recv, fwd_send, ck_send, ck_recv, q_send, q_recv, kv_send, kv_recv,
+    wo_send, wo_recv, ot_send, ot_recv, st_send, st_recv, hop_send_sem, hop_recv_sem, dir_send, dir_recv,
+    sum_send, sum_recv, mate_send, mate_recv,
 ):
     span = lax.axis_index("span")
     tensor = lax.axis_index("tensor")
@@ -86,7 +86,7 @@
 
     barrier = pltpu.get_barrier_semaphore()
     peers = [sibling]
-    peers += [chip_device(dl, dy, core) for dl, dy in CHIP_STEPS]
+    peers += [chip_device(dl, dy, core) for dl, dy in NEAR]
     peers += [x_device(dx) for dx in (1, 2, 3)]
     peers += [z_device(dz, c) for dz in (1, 2, 3) for c in (0, 1)]
     for device in peers:
@@ -117,7 +117,7 @@
         waits.append(copy)
 
     own_rows = x_buf.at[tensor]
-    for k, (dl, dy) in enumerate(CHIP_STEPS):
+    for k, (dl, dy) in enumerate(NEAR):
         send(own_rows, own_rows, lat_send.at[k], lat_recv.at[tensor], chip_device(dl, dy, core))
     send(own_rows, own_rows, fwd_send.at[7], lat_recv.at[tensor], sibling)
 
@@ -157,22 +157,35 @@
         arrived((first + 1) * 2 + other)
         normalise_pair(first, other)
 
-    for g, (dl, dp) in enumerate(GROUPS):
-        first = group_chip(dl, dp)
-        if g == 0:
-            mate = first + (1 - y % 2)
-            members = [mate]
-        else:
-            members = [first, first + 1]
-        for m, member in enumerate(members):
-            arrived(member * 2 + core)
-            piece = x_buf.at[member * 2 + core]
-            k = 0 if g == 0 else 2 * g - 1 + m
-            send(piece, piece, fwd_send.at[k], lat_recv.at[member * 2 + core], sibling)
+    def pass_on(index, k):
+        piece = x_buf.at[index]
+        send(piece, piece, fwd_send.at[k], lat_recv.at[index], sibling)
+
+    for k, (dl, dy) in enumerate(NEAR):
+        index = chip_at(dl, dy) * 2 + core
+        arrived(index)
+        if dy:
+            side = 0 if dy == 3 else 1
+            piece = x_buf.at[index, :, side * HALF : (side + 1) * HALF]
+            send(piece, piece, far_send.at[2 * dl + side], far_recv.at[2 * dl + side], chip_device(0, 4 - dy, core))
+        pass_on(index, k)
+    near = [group_chip(dl, 0) for dl in range(2)]
+    far = [group_chip(dl, 1) for dl in range(2)]
+    for first in near:
         normalise_pair(first, core)
-        if g > 0:
-            sibling_pair(group_chip(*GROUPS[g - 1]))
-    sibling_pair(group_chip(*GROUPS[3]))
+    for first in near:
+        sibling_pair(first)
+    for dl, first in enumerate(far):
+        index = chip_at(dl, 2) * 2 + core
+        for side in range(2):
+            piece = x_buf.at[index, :, side * HALF : (side + 1) * HALF]
+            remote(piece, piece, far_send.at[0], far_recv.at[2 * dl + side], sibling).wait_recv()
+        pass_on(index, 5 + dl)
+        normalise_pair(first, core)
+    for first in far:
+        sibling_pair(first)
+
+    always = jnp.full((1, 1), span, jnp.int32) >= 0
 
     def project(which):
         sums = [None, None]
@@ -180,7 +193,7 @@
             depth = slice(n // 2 * 256 + n % 2 * HALF, (n // 2 + 1) * 256 + n % 2 * HALF)
             part = jnp.dot(lhs[:, depth], w_in[which, depth], preferred_element_type=F32)
             sums[n % 2] = part if sums[n % 2] is None else sums[n % 2] + part
-        return (sums[0] + sums[1]).astype(BF16)
+        return (sums[0] + jnp.where(always, sums[1], 0.0)).astype(BF16)
 
     loads[4].wait()
     queries = project(0)
@@ -247,13 +260,21 @@
             best = jnp.max(s.reshape(256 // ROWS, ROWS, width), axis=0)
             top = best if top is None else jnp.maximum(top, best)
         top = jnp.max(top, axis=0, keepdims=True)
-        acc = total = None
+        peak = jnp.broadcast_to(top, (ROWS, width))
+        step = 128
+
+        def weigh(n, total):
+            rows = pl.ds(pl.multiple_of(n * step, step), step)
+            p = jnp.exp2((scores[rows].reshape(step // ROWS, ROWS, width) - peak) * SCALE2)
+            probs[rows] = p.reshape(step, width).astype(BF16)
+            return total + jnp.sum(p, axis=0)
+
+        total = lax.fori_loop(0, KEYS // step, weigh, jnp.zeros((ROWS, width), F32))
+        sums = [None, None]
         for j in range(chunks):
-            p = jnp.exp2((scores[j * 256 : (j + 1) * 256] - top) * SCALE2)
-            share = jnp.sum(p.reshape(256 // ROWS, ROWS, width), axis=0)
-            part = jnp.dot(value_chunk(h, j), p.astype(BF16), preferred_element_type=F32)
-            total = share if total is None else total + share
-            acc = part if acc is None else acc + part
+            part = jnp.dot(value_chunk(h, j), probs[j * 256 : (j + 1) * 256], preferred_element_type=F32)
+            sums[j % 2] = part if sums[j % 2] is None else sums[j % 2] + part
+        acc = sums[0] + jnp.where(always, sums[1], 0.0)
         total = jnp.sum(total, axis=0, keepdims=True)
         lse = top * SCALE2 + jnp.log2(total)
         acc = acc / total
@@ -283,7 +304,7 @@
                 results += attend(h, zqs)
             part, stat = results[k]
             rows = CHIPS * ROWS
-            s_send[h, zq] = jnp.broadcast_to(stat, (8, SPAN))
+            s_send[h, zq] = stat
             o_send[h, zq, 0] = part[:rows]
             o_send[h, zq, 1] = part[rows:]
             for c in range(2):
@@ -320,7 +341,7 @@
                     remote(s_recv.at[h, zs, cs], s_recv.at[h, zs, cs], st_send.at[0], st_recv.at[slot], sibling).wait_recv()
         for cs in range(2):
             lses = [
-                jnp.sum(jnp.where(mine, s_recv[h, zs, cs, 0:1, :], 0.0), axis=1, keepdims=True) for zs in range(ZN)
+                jnp.sum(jnp.where(mine, s_recv[h, zs, cs], 0.0), axis=1, keepdims=True) for zs in range(ZN)
             ]
             best = jnp.maximum(jnp.maximum(lses[0], lses[1]), jnp.maximum(lses[2], lses[3]))
             shares = [jnp.exp2(value - best) for value in lses]
@@ -329,29 +350,69 @@
             att[:, (2 * cs + h) * HD : (2 * cs + h + 1) * HD] = (summed / whole).astype(BF16)
 
     remote(w_o.at[other], w_o.at[other], wo_send, wo_recv, sibling).wait_recv()
+    def halves(part, side):
+        return pl.ds(part * WIDTH + side * (WIDTH // 2), WIDTH // 2)
+
     for part in range(PARTS):
         cols = pl.ds(part * WIDTH, WIDTH)
-        value = jnp.dot(att[:, : 2 * HD], w_o[0, :, cols], preferred_element_type=F32) + jnp.dot(
-            att[:, 2 * HD :], w_o[1, :, cols], preferred_element_type=F32
+        for n in range(WIDTH // 256):
+            sub = pl.ds(part * WIDTH + n * 256, 256)
+            value = jnp.dot(att[:, : 2 * HD], w_o[0, :, sub], preferred_element_type=F32) + jnp.dot(
+                att[:, 2 * HD :], w_o[1, :, sub], preferred_element_type=F32
+            )
+            p_send[:, :, sub] = value.reshape(CHIPS, ROWS, 256).astype(BF16)
+        for dl in range(2):
+            for side in range(2):
+                n = 4 * part + 2 * dl + side
+                send(
+                    p_send.at[chip_at(dl, 2), :, halves(part, side)], hop_recv.at[n],
+                    hop_send_sem.at[n], hop_recv_sem.at[n], chip_device(0, 1 if side == 0 else 3, core),
+                )
+        for dl in range(2):
+            for side in range(2):
+                half = halves(part, 1 - side)
+                dy = 1 if side == 0 else 3
+                n = 4 * part + 2 * dl + side
+                send(
+                    p_send.at[chip_at(dl, dy), :, half], p_recv.at[chip, :, half],
+                    dir_send.at[n], dir_recv.at[n], chip_device(dl, dy, core),
+                )
+        send(
+            p_send.at[chip_at(1, 0), :, cols], p_recv.at[chip, :, cols], mate_send.at[part], mate_recv.at[part],
+            chip_device(1, 0, core),
         )
-        p_send[:, :, cols] = value.reshape(CHIPS, ROWS, WIDTH).astype(BF16)
-        for k, (dl, dy) in enumerate(CHIP_STEPS):
-            send(
-                p_send.at[chip_at(dl, dy), :, cols], p_recv.at[chip, :, cols], pr_send.at[7 * part + k],
-                pr_recv.at[8 * part + chip], chip_device(dl, dy, core),
-            )
+
+    for part in range(PARTS):
+        for dl in range(2):
+            for side in range(2):
+                half = halves(part, side)
+                n = 4 * part + 2 * dl + side
+                held = hop_recv.at[n]
+                remote(held, held, hop_send_sem.at[0], hop_recv_sem.at[n], sibling).wait_recv()
+                dy = 1 if side == 0 else 3
+                index = chip_at(dl, dy)
+                added = p_send[index, :, half].astype(F32) + held[...].astype(F32)
+                p_sum[n] = added.astype(BF16)
+                send(
+                    p_sum.at[n], p_recv.at[chip, :, half], sum_send.at[n], sum_recv.at[n], chip_device(dl, dy, core),
+                )
 
     gate = mod[2, pl.ds(level, 1), :]
     for part in range(PARTS):
         cols = pl.ds(part * WIDTH, WIDTH)
         total = p_send[chip, :, cols].astype(F32)
-        for dl, dy in CHIP_STEPS:
-            source = chip_at(dl, dy)
-            remote(
-                p_recv.at[source, :, cols], p_recv.at[source, :, cols], pr_send.at[0], pr_recv.at[8 * part + source],
-                sibling,
-            ).wait_recv()
-            total = total + p_recv[source, :, cols].astype(F32)
+        mate = p_recv.at[chip_at(1, 0), :, cols]
+        remote(mate, mate, mate_send.at[0], mate_recv.at[part], sibling).wait_recv()
+        total = total + mate[...].astype(F32)
+        for dl in range(2):
+            for side in range(2):
+                source = chip_at(dl, 3 if side == 0 else 1)
+                n = 4 * part + 2 * dl + side
+                late = p_recv.at[source, :, halves(part, side)]
+                early = p_recv.at[source, :, halves(part, 1 - side)]
+                remote(early, early, dir_send.at[0], dir_recv.at[n], sibling).wait_recv()
+                remote(late, late, sum_send.at[0], sum_recv.at[n], sibling).wait_recv()
+                total = total + p_recv[source, :, cols].astype(F32)
         out_ref[:, cols] = (gate[:, part * WIDTH : (part + 1) * WIDTH] * total).astype(BF16)
 
     for copy in waits:
@@ -389,16 +450,21 @@
             pltpu.VMEM((ZN, XN, ROWS, SPAN), F32),
             pltpu.VMEM((CACHE, 2 * HD), BF16),
             pltpu.VMEM((KEYS, 2 * SPAN), F32),
+            pltpu.VMEM((KEYS, 2 * SPAN), BF16),
             pltpu.VMEM((2, ZN, 2, rows, HD), BF16),
             pltpu.VMEM((2, ZN, 2, rows, HD), BF16),
-            pltpu.VMEM((2, ZN, 8, SPAN), F32),
-            pltpu.VMEM((2, ZN, 2, 8, SPAN), F32),
+            pltpu.VMEM((2, ZN, 1, SPAN), F32),
+            pltpu.VMEM((2, ZN, 2, 1, SPAN), F32),
             pltpu.VMEM((rows, 4 * HD), BF16),
             pltpu.VMEM((CHIPS, ROWS, D), BF16),
             pltpu.VMEM((CHIPS, ROWS, D), BF16),
+            pltpu.VMEM((4 * PARTS, ROWS, WIDTH // 2), BF16),
+            pltpu.VMEM((4 * PARTS, ROWS, WIDTH // 2), BF16),
             dma((11,)),
-            dma((7,)),
+            dma((5,)),
             dma((16,)),
+            dma((4,)),
+            dma((4,)),
             dma((8,)),
             dma((6,)),
             dma((8,)),
@@ -412,8 +478,14 @@
             dma((16,)),
             dma((14,)),
             dma((16,)),
-            dma((7 * PARTS,)),
-            dma((8 * PARTS,)),
+            dma((4 * PARTS,)),
+            dma((4 * PARTS,)),
+            dma((4 * PARTS,)),
+            dma((4 * PARTS,)),
+            dma((4 * PARTS,)),
+            dma((4 * PARTS,)),
+            dma((PARTS,)),
+            dma((PARTS,)),
         ],
         compiler_params=pltpu.CompilerParams(
             collective_id=0, has_side_effects=True, vmem_limit_bytes=60 * 1024 * 1024

time: 56.2 us -> 53.2 us (0.947)
  Pallas kernels: 53.2 us -> 50 us
    pallas_call x1, Pallas kernels: 53.2 us -> 50 us  [body(): pl.pallas_call(kernel, out_shape=jax.ShapeDtypeStruct((ROWS, D), BF16), i...]
where the time goes in v3:
time: 53.2 us; the launch traced here: 52.8 us
  Pallas kernels  50 us (94%)
  local copies, waits for them, and re-layouts  1.53 us (3%)
  between operations  1.3 us (2%)
    pallas_call x1, Pallas kernels, body(): pl.pallas_call(kernel, out_shape=jax.ShapeDtypeStruct((ROWS, D), BF16), i...  50 us
    unnamed x1, local copies, waits for them, and re-layouts  1.53 us

profile of v3, /device:TPU:1, one launch (start us, length us, event | category | flops | bytes accessed | tf_op | source)
XLA Modules:
  0.0 52.8 jit_solution(13608180460975031187)
XLA Ops:
  1.3 50.0 %attention_step.1 = bf16[8,5120]{1,0:T(8,128)(2,1)} custom-call(bf16[8,5120]{1,0:T(8,128)(2,1)} %latents.1, f32[3,4,5120]{2,1,0:T(4,128)} %bitcast.1, bf16[5120,256]{1,0:T(8,128)(2,1)} %w_query.1, bf16[5120,256]{1,0:T(8,128)(2,1)} %w_key.1, bf16[5120,256]{1,0:T(8,128)(2,1)} %w_value.1, bf16[256,5120]{1,0:T(8,128)(2,1)} %w_out.1, bf16[256,256]{1,0:T(8,128)(2,1)} %cache_k.1, ...), custom_call_target="tpu_custom_call" | custom-call | tf_op jit(solution)/shard_map/attention_step/pallas_call | solution.py:428
  51.3 1.5 %copy.15 = bf16[8,5120]{1,0:T(8,128)(2,1)} copy(bf16[8,5120]{1,0:T(8,128)(2,1)} %attention_step.1) | data formatting | bytes 163840

commit v4 on v3

--- a/solution.py
+++ b/solution.py
@@ -24,14 +24,15 @@
 SPAN = 128
 KEYS = XN * (CACHE + SPAN)
 NEAR = ((0, 1), (0, 3), (1, 1), (1, 3), (1, 0))
-PARTS = 4
+PLANE = 64
+PARTS = 1
 WIDTH = D // PARTS
 
 
 def kernel(
     latents, modulation, w_query, w_key, w_value, w_out, cache_k, cache_v, level_index, rotation, cached_tokens,
     out_ref,
-    level_s, rot_s, live_s, x_buf, lhs, mod, scale_rows, shift_rows, w_in, w_o, ck, cv, nk, nv, qb, slot_bias, span_bias, v_raw, scores, probs,
+    level_s, rot_s, live_s, x_buf, lhs, mod, scale_rows, shift_rows, w_in, w_o, ck, cv, kv, nv, qb, slot_bias, span_bias, v_raw, scores, probs,
     o_send, o_recv, s_send, s_recv, att, p_send, p_recv, p_sum, hop_recv,
     load_sem, lat_send, lat_recv, far_send, far_recv, fwd_send, ck_send, ck_recv, q_send, q_recv, kv_send, kv_recv,
     wo_send, wo_recv, ot_send, ot_recv, st_send, st_recv, hop_send_sem, hop_recv_sem, dir_send, dir_recv,
@@ -146,7 +147,7 @@
         rows = jnp.concatenate(
             [normalised(first_chip * 2 + c), normalised((first_chip + 1) * 2 + c)], axis=0
         )
-        start = pl.multiple_of(c * (CHIPS * ROWS) + first_chip * ROWS, 16)
+        start = pl.multiple_of((first_chip // YN) * PLANE + c * (PLANE // 2) + (first_chip % YN) * ROWS, 16)
         lhs[pl.ds(start, 16), :] = rows.astype(BF16)
 
     def group_chip(dl, dp):
@@ -169,58 +170,64 @@
             piece = x_buf.at[index, :, side * HALF : (side + 1) * HALF]
             send(piece, piece, far_send.at[2 * dl + side], far_recv.at[2 * dl + side], chip_device(0, 4 - dy, core))
         pass_on(index, k)
-    near = [group_chip(dl, 0) for dl in range(2)]
-    far = [group_chip(dl, 1) for dl in range(2)]
-    for first in near:
-        normalise_pair(first, core)
-    for first in near:
-        sibling_pair(first)
-    for dl, first in enumerate(far):
+    always = jnp.full((1, 1), span, jnp.int32) >= 0
+
+    def project(which, plane):
+        rows = pl.ds(pl.multiple_of(plane * PLANE, PLANE), PLANE)
+        sums = [None, None]
+        for n in range(D // 256):
+            depth = slice(n // 2 * 256 + n % 2 * HALF, (n // 2 + 1) * 256 + n % 2 * HALF)
+            part = jnp.dot(lhs[rows, depth], w_in[which, depth], preferred_element_type=F32)
+            sums[n % 2] = part if sums[n % 2] is None else sums[n % 2] + part
+        return (sums[0] + jnp.where(always, sums[1], 0.0)).astype(BF16)
+
+    def far_rows(dl):
         index = chip_at(dl, 2) * 2 + core
         for side in range(2):
             piece = x_buf.at[index, :, side * HALF : (side + 1) * HALF]
             remote(piece, piece, far_send.at[0], far_recv.at[2 * dl + side], sibling).wait_recv()
         pass_on(index, 5 + dl)
-        normalise_pair(first, core)
-    for first in far:
-        sibling_pair(first)
-
-    always = jnp.full((1, 1), span, jnp.int32) >= 0
-
-    def project(which):
-        sums = [None, None]
-        for n in range(D // 256):
-            depth = slice(n // 2 * 256 + n % 2 * HALF, (n // 2 + 1) * 256 + n % 2 * HALF)
-            part = jnp.dot(lhs[:, depth], w_in[which, depth], preferred_element_type=F32)
-            sums[n % 2] = part if sums[n % 2] is None else sums[n % 2] + part
-        return (sums[0] + jnp.where(always, sums[1], 0.0)).astype(BF16)
-
-    loads[4].wait()
-    queries = project(0)
-    for h in range(2):
-        qb[h, zh] = queries[:, h * HD : (h + 1) * HD]
-    for h in range(2):
-        for k, dz in enumerate((2, 1, 3)):
-            send(qb.at[h, zh], qb.at[h, zh], q_send.at[3 * h + k], q_recv.at[4 * h + zh], z_device(dz, core))
-
-    def send_rows(buf, v, h):
-        for k, dx in enumerate((1, 3, 2)):
-            send(
-                buf.at[h, x], buf.at[h, x], kv_send.at[3 * (2 * v + h) + k], kv_recv.at[4 * (2 * v + h) + x], x_device(dx)
-            )
-
-    loads[5].wait()
-    keys = project(1)
-    for h in range(2):
-        nk[h, x] = keys[:, h * HD : (h + 1) * HD]
-    send_rows(nk, 0, 0)
-    loads[6].wait()
-    values = project(2)
-    for h in range(2):
-        nv[h, x] = values[:, h * HD : (h + 1) * HD].T
-    send_rows(nv, 1, 0)
-    send_rows(nk, 0, 1)
-    send_rows(nv, 1, 1)
+
+    for dl in range(2):
+        plane = (zl + dl) % 2
+        near, far = group_chip(dl, 0), group_chip(dl, 1)
+        normalise_pair(near, core)
+        if dl == 0:
+            far_rows(0)
+        sibling_pair(near)
+        if dl == 1:
+            far_rows(1)
+        normalise_pair(far, core)
+        sibling_pair(far)
+        if dl == 0:
+            loads[4].wait()
+        queries = project(0, plane)
+        for h in range(2):
+            qb[zh, plane, h] = queries[:, h * HD : (h + 1) * HD]
+        if dl == 0:
+            for k, dz in enumerate((2, 1, 3)):
+                rows = qb.at[zh, plane]
+                send(rows, rows, q_send.at[k], q_recv.at[zh], z_device(dz, core))
+            loads[5].wait()
+            loads[6].wait()
+        else:
+            for h in range(2):
+                for k, dz in enumerate((2, 1, 3)):
+                    rows = qb.at[zh, plane, h]
+                    send(rows, rows, q_send.at[3 + 3 * h + k], q_recv.at[ZN + ZN * h + zh], z_device(dz, core))
+        for v in range(2):
+            value = project(1 + v, plane)
+            for h in range(2):
+                kv[x, plane, h, v] = value[:, h * HD : (h + 1) * HD]
+        if dl == 0:
+            for k, dx in enumerate((2, 1, 3)):
+                rows = kv.at[x, plane]
+                send(rows, rows, kv_send.at[k], kv_recv.at[x], x_device(dx))
+        else:
+            for h in range(2):
+                for k, dx in enumerate((2, 1, 3)):
+                    rows = kv.at[x, plane, h]
+                    send(rows, rows, kv_send.at[3 + 3 * h + k], kv_recv.at[XN + XN * h + x], x_device(dx))
     loads[7].wait()
     send(w_o.at[core], w_o.at[core], wo_send, wo_recv, sibling)
 
@@ -228,13 +235,13 @@
         if j < XN:
             return ck[j, :, h * HD : (h + 1) * HD]
         j -= XN
-        return nk[h, 2 * j : 2 * j + 2].reshape(2 * SPAN, HD)
+        return jnp.concatenate([kv[xk, :, h, 0].reshape(SPAN, HD) for xk in (2 * j, 2 * j + 1)], axis=0)
 
     def value_chunk(h, j):
         if j < XN:
             return cv[j, h * HD : (h + 1) * HD, :]
         j -= XN
-        return jnp.concatenate([nv[h, 2 * j], nv[h, 2 * j + 1]], axis=1)
+        return jnp.concatenate([nv[2 * j], nv[2 * j + 1]], axis=1)
 
     def mask_chunk(zqs, j):
         if j < XN:
@@ -251,7 +258,7 @@
 
     def attend(h, zqs):
         width = len(zqs) * SPAN
-        q = jnp.concatenate([qb[h, zq] for zq in zqs], axis=0)
+        q = jnp.concatenate([qb[zq, :, h].reshape(SPAN, HD) for zq in zqs], axis=0)
         top = None
         for j in range(chunks):
             s = lax.dot_general(key_chunk(h, j), q, (((1,), (1,)), ((), ())), preferred_element_type=F32)
@@ -290,23 +297,33 @@
             if h == 0:
                 remote(ck.at[xk], ck.at[xk], ck_send.at[0], ck_recv.at[2 * xk], sibling).wait_recv()
                 remote(cv.at[xk], cv.at[xk], ck_send.at[0], ck_recv.at[2 * xk + 1], sibling).wait_recv()
-            remote(nk.at[h, xk], nk.at[h, xk], kv_send.at[0], kv_recv.at[4 * h + xk], sibling).wait_recv()
-            remote(nv.at[h, xk], nv.at[h, xk], kv_send.at[0], kv_recv.at[8 + 4 * h + xk], sibling).wait_recv()
+                rows = kv.at[xk, zl]
+                remote(rows, rows, kv_send.at[0], kv_recv.at[xk], sibling).wait_recv()
+            rows = kv.at[xk, 1 - zl, h]
+            remote(rows, rows, kv_send.at[0], kv_recv.at[XN + XN * h + xk], sibling).wait_recv()
+        for xk in range(XN):
+            nv[xk] = kv[xk, :, h, 1].reshape(SPAN, HD).T
         results = []
-        for k, dz in enumerate((1, 3, 2, 0)):
+        for k, dz in enumerate((2, 1, 3, 0)):
             zq = (zh + dz) % ZN
             if k % 2 == 0:
-                pair = [1, 3] if k == 0 else [2, 0]
+                pair = [2, 1] if k == 0 else [3, 0]
                 zqs = [(zh + d) % ZN for d in pair]
                 for d, z in zip(pair, zqs):
                     if d:
-                        remote(qb.at[h, z], qb.at[h, z], q_send.at[0], q_recv.at[4 * h + z], sibling).wait_recv()
+                        if h == 0:
+                            rows = qb.at[z, zl]
+                            remote(rows, rows, q_send.at[0], q_recv.at[z], sibling).wait_recv()
+                        rows = qb.at[z, 1 - zl, h]
+                        remote(rows, rows, q_send.at[0], q_recv.at[ZN + ZN * h + z], sibling).wait_recv()
                 results += attend(h, zqs)
             part, stat = results[k]
-            rows = CHIPS * ROWS
             s_send[h, zq] = stat
-            o_send[h, zq, 0] = part[:rows]
-            o_send[h, zq, 1] = part[rows:]
+            for c in range(2):
+                quarter = PLANE // 2
+                for plane in range(2):
+                    start = plane * PLANE + c * quarter
+                    o_send[h, zq, c, plane * quarter : (plane + 1) * quarter] = part[start : start + quarter]
             for c in range(2):
                 if dz:
                     n = 6 * h + 2 * k + c
@@ -327,9 +344,9 @@
                 s_recv[h, zh, core] = s_send[h, zh]
 
     rows = CHIPS * ROWS
-    mine = lax.broadcasted_iota(jnp.int32, (rows, SPAN), 1) == core * rows + lax.broadcasted_iota(
-        jnp.int32, (rows, SPAN), 0
-    )
+    place = lax.broadcasted_iota(jnp.int32, (rows, SPAN), 0)
+    place = jnp.where(place < PLANE // 2, place, place + PLANE // 2) + core * (PLANE // 2)
+    mine = lax.broadcasted_iota(jnp.int32, (rows, SPAN), 1) == place
     for h in range(2):
         for dz in (0, 1, 3, 2):
             zs = (zh + dz) % ZN
@@ -443,9 +460,9 @@
             pltpu.VMEM((2, 2 * HD, D), BF16),
             pltpu.VMEM((XN, CACHE, 2 * HD), BF16),
             pltpu.VMEM((XN, 2 * HD, CACHE), BF16),
-            pltpu.VMEM((2, XN, SPAN, HD), BF16),
-            pltpu.VMEM((2, XN, HD, SPAN), BF16),
-            pltpu.VMEM((2, ZN, SPAN, HD), BF16),
+            pltpu.VMEM((XN, 2, 2, 2, PLANE, HD), BF16),
+            pltpu.VMEM((XN, HD, SPAN), BF16),
+            pltpu.VMEM((ZN, 2, 2, PLANE, HD), BF16),
             pltpu.VMEM((XN * CACHE, SPAN), F32),
             pltpu.VMEM((ZN, XN, ROWS, SPAN), F32),
             pltpu.VMEM((CACHE, 2 * HD), BF16),
@@ -468,10 +485,10 @@
             dma((8,)),
             dma((6,)),
             dma((8,)),
-            dma((6,)),
-            dma((8,)),
+            dma((9,)),
             dma((12,)),
-            dma((16,)),
+            dma((9,)),
+            dma((12,)),
             dma(()),
             dma(()),
             dma((14,)),

time: 53.2 us -> 53.3 us (level)
  no operation moved by 1% of the time
where the time goes in v4:
time: 53.3 us; the launch traced here: 52.9 us
  Pallas kernels  50.1 us (94%)
  local copies, waits for them, and re-layouts  1.53 us (3%)
  between operations  1.3 us (2%)
    pallas_call x1, Pallas kernels, body(): pl.pallas_call(kernel, out_shape=jax.ShapeDtypeStruct((ROWS, D), BF16), i...  50.1 us
    unnamed x1, local copies, waits for them, and re-layouts  1.53 us

profile of v4, /device:TPU:1, one launch (start us, length us, event | category | flops | bytes accessed | tf_op | source)
XLA Modules:
  0.0 52.9 jit_solution(9833718554928780347)
XLA Ops:
  1.3 50.1 %attention_step.1 = bf16[8,5120]{1,0:T(8,128)(2,1)} custom-call(bf16[8,5120]{1,0:T(8,128)(2,1)} %latents.1, f32[3,4,5120]{2,1,0:T(4,128)} %bitcast.1, bf16[5120,256]{1,0:T(8,128)(2,1)} %w_query.1, bf16[5120,256]{1,0:T(8,128)(2,1)} %w_key.1, bf16[5120,256]{1,0:T(8,128)(2,1)} %w_value.1, bf16[256,5120]{1,0:T(8,128)(2,1)} %w_out.1, bf16[256,256]{1,0:T(8,128)(2,1)} %cache_k.1, ...), custom_call_target="tpu_custom_call" | custom-call | tf_op jit(solution)/shard_map/attention_step/pallas_call | solution.py:445
  51.4 1.5 %copy.15 = bf16[8,5120]{1,0:T(8,128)(2,1)} copy(bf16[8,5120]{1,0:T(8,128)(2,1)} %attention_step.1) | data formatting | bytes 163840

commit v5 on v3

--- a/solution.py
+++ b/solution.py
@@ -24,7 +24,7 @@
 SPAN = 128
 KEYS = XN * (CACHE + SPAN)
 NEAR = ((0, 1), (0, 3), (1, 1), (1, 3), (1, 0))
-PARTS = 4
+PARTS = 2
 WIDTH = D // PARTS
 
 
@@ -66,6 +66,14 @@
             src_ref=src, dst_ref=dst, send_sem=send, recv_sem=recv, device_id=device, device_id_type=MESH
         )
 
+    barrier = pltpu.get_barrier_semaphore()
+    peers = [z_device(dz, c) for dz in (2, 1, 3) for c in (0, 1)]
+    peers += [chip_device(dl, dy, core) for dl, dy in NEAR]
+    peers += [x_device(dx) for dx in (2, 1, 3)]
+    peers += [sibling]
+    for device in peers:
+        pl.semaphore_signal(barrier, inc=1, device_id=device, device_id_type=MESH)
+
     scalars = [
         pltpu.make_async_copy(level_index, level_s, load_sem.at[8]),
         pltpu.make_async_copy(rotation, rot_s, load_sem.at[9]),
@@ -83,14 +91,6 @@
     ]
     for copy in loads[:1] + scalars + loads[1:]:
         copy.start()
-
-    barrier = pltpu.get_barrier_semaphore()
-    peers = [sibling]
-    peers += [chip_device(dl, dy, core) for dl, dy in NEAR]
-    peers += [x_device(dx) for dx in (1, 2, 3)]
-    peers += [z_device(dz, c) for dz in (1, 2, 3) for c in (0, 1)]
-    for device in peers:
-        pl.semaphore_signal(barrier, inc=1, device_id=device, device_id_type=MESH)
 
     for copy in scalars:
         copy.wait()
@@ -204,7 +204,7 @@
             send(qb.at[h, zh], qb.at[h, zh], q_send.at[3 * h + k], q_recv.at[4 * h + zh], z_device(dz, core))
 
     def send_rows(buf, v, h):
-        for k, dx in enumerate((1, 3, 2)):
+        for k, dx in enumerate((2, 1, 3)):
             send(
                 buf.at[h, x], buf.at[h, x], kv_send.at[3 * (2 * v + h) + k], kv_recv.at[4 * (2 * v + h) + x], x_device(dx)
             )
@@ -255,7 +255,7 @@
         top = None
         for j in range(chunks):
             s = lax.dot_general(key_chunk(h, j), q, (((1,), (1,)), ((), ())), preferred_element_type=F32)
-            s = s + mask_chunk(zqs, j)
+            s = s * SCALE2 + mask_chunk(zqs, j)
             scores[j * 256 : (j + 1) * 256] = s
             best = jnp.max(s.reshape(256 // ROWS, ROWS, width), axis=0)
             top = best if top is None else jnp.maximum(top, best)
@@ -265,7 +265,7 @@
 
         def weigh(n, total):
             rows = pl.ds(pl.multiple_of(n * step, step), step)
-            p = jnp.exp2((scores[rows].reshape(step // ROWS, ROWS, width) - peak) * SCALE2)
+            p = jnp.exp2(scores[rows].reshape(step // ROWS, ROWS, width) - peak)
             probs[rows] = p.reshape(step, width).astype(BF16)
             return total + jnp.sum(p, axis=0)
 
@@ -276,7 +276,7 @@
             sums[j % 2] = part if sums[j % 2] is None else sums[j % 2] + part
         acc = sums[0] + jnp.where(always, sums[1], 0.0)
         total = jnp.sum(total, axis=0, keepdims=True)
-        lse = top * SCALE2 + jnp.log2(total)
+        lse = top + jnp.log2(total)
         acc = acc / total
         out = []
         for n in range(len(zqs)):
@@ -293,10 +293,10 @@
             remote(nk.at[h, xk], nk.at[h, xk], kv_send.at[0], kv_recv.at[4 * h + xk], sibling).wait_recv()
             remote(nv.at[h, xk], nv.at[h, xk], kv_send.at[0], kv_recv.at[8 + 4 * h + xk], sibling).wait_recv()
         results = []
-        for k, dz in enumerate((1, 3, 2, 0)):
+        for k, dz in enumerate((2, 1, 3, 0)):
             zq = (zh + dz) % ZN
             if k % 2 == 0:
-                pair = [1, 3] if k == 0 else [2, 0]
+                pair = [2, 1] if k == 0 else [3, 0]
                 zqs = [(zh + d) % ZN for d in pair]
                 for d, z in zip(pair, zqs):
                     if d:

time: 53.2 us -> 52.8 us (level)
  no operation moved by 1% of the time
where the time goes in v5:
time: 52.8 us; the launch traced here: 52.7 us
  Pallas kernels  49.8 us (94%)
  local copies, waits for them, and re-layouts  1.53 us (3%)
  between operations  1.3 us (2%)
    pallas_call x1, Pallas kernels, body(): pl.pallas_call(kernel, out_shape=jax.ShapeDtypeStruct((ROWS, D), BF16), i...  49.8 us
    unnamed x1, local copies, waits for them, and re-layouts  1.53 us

profile of v5, /device:TPU:1, one launch (start us, length us, event | category | flops | bytes accessed | tf_op | source)
XLA Modules:
  0.0 52.7 jit_solution(11309335007832092330)
XLA Ops:
  1.3 49.8 %attention_step.1 = bf16[8,5120]{1,0:T(8,128)(2,1)} custom-call(bf16[8,5120]{1,0:T(8,128)(2,1)} %latents.1, f32[3,4,5120]{2,1,0:T(4,128)} %bitcast.1, bf16[5120,256]{1,0:T(8,128)(2,1)} %w_query.1, bf16[5120,256]{1,0:T(8,128)(2,1)} %w_key.1, bf16[5120,256]{1,0:T(8,128)(2,1)} %w_value.1, bf16[256,5120]{1,0:T(8,128)(2,1)} %w_out.1, bf16[256,256]{1,0:T(8,128)(2,1)} %cache_k.1, ...), custom_call_target="tpu_custom_call" | custom-call | tf_op jit(solution)/shard_map/attention_step/pallas_call | solution.py:428
  51.1 1.5 %copy.15 = bf16[8,5120]{1,0:T(8,128)(2,1)} copy(bf16[8,5120]{1,0:T(8,128)(2,1)} %attention_step.1) | data formatting | bytes 163840
